TPU v7x, 128 devices: a whole 4x4x4 slice. The times are simulated.
128 devices in a mesh: depth: 2 (over core), row: 16 (over z, x), col: 4 (over y).
Axes of the slice: x: 4, y: 4, z: 4, core: 2. Of those that a mesh axis runs over, the one named last changes fastest.
Arguments:
- right_side: bfloat16 [4, 16, 8, 128, 512], P(None, 'row', ('depth', 'col')), may hold values from -6 to 6
- inverse_diag: bfloat16 [4, 16, 8, 1, 128, 128], P(None, 'row', ('depth', 'col')), may hold values from -2 to 2.5, as said below
- coupling: bfloat16 [3, 16, 1024, 8, 2048], P(None, 'row', None, ('depth', 'col')), may hold values from -0.0625 to 0.0625
- pattern: int32 [3, 16, 8, 8, 16], P(None, 'row', None, ('depth', 'col')), may hold values 0 or 1
Outputs:
- forward_solution: bfloat16 [4, 16, 8, 128, 512], P(None, 'row', ('depth', 'col'))
- solution: bfloat16 [4, 16, 8, 128, 512], P(None, 'row', ('depth', 'col'))
Inputs may be any that keep to these rules, and one draw needn't show every extreme that they name: `inverse_diag`: each block is lower triangular with positive diagonal.
All inputs are finite; a program needn't handle non-finite values. No bound on the sum of `pattern` on one device may be relied on, other than what follows from the above.
Results may differ from a plain program's by a relative error of at most 0.025.
Values may be sent and summed in bfloat16 or wider, within the bound.
A program may use at most 128 MiB of HBM per device.

v0:
```python
import jax
import jax.numpy as jnp
from jax import lax
from jax.sharding import PartitionSpec as P


def apply_inverse(inverse, vector, transposed):
    blocks_in = vector.reshape(inverse.shape[0], inverse.shape[1], vector.shape[-1])
    einsum_form = "tji,tjn->tin" if transposed else "tij,tjn->tin"
    result = jnp.einsum(einsum_form, inverse, blocks_in, preferred_element_type=jnp.float32)
    return result.astype(jnp.bfloat16).reshape(vector.shape)


def lift_upward(masked, share_in):
    portion = lax.all_gather(share_in, "row", axis=0, tiled=True)
    span_rows = portion.shape[0] * portion.shape[2]
    return jnp.dot(
        masked, portion.reshape(span_rows, portion.shape[-1]), preferred_element_type=jnp.float32
    )


def carry_downward(masked, share_in):
    portion = lax.all_gather(share_in, ("depth", "col"), axis=1, tiled=True)
    span_rows = portion.shape[1] * portion.shape[2]
    return lax.dot_general(
        masked,
        portion.reshape(span_rows, portion.shape[-1]),
        (((0,), (0,)), ((), ())),
        preferred_element_type=jnp.float32,
    )


def forward_sum(partial_value, share_rows):
    blocks = partial_value.reshape(
        lax.axis_size(("depth", "col")), share_rows, partial_value.shape[-1]
    )
    summed = lax.psum(blocks.astype(jnp.bfloat16), ("depth", "col")).astype(jnp.float32)
    return lax.dynamic_index_in_dim(summed, lax.axis_index(("depth", "col")), 0, keepdims=False)


def backward_sum(partial_value, share_rows):
    blocks = partial_value.reshape(lax.axis_size("row"), share_rows, partial_value.shape[-1])
    summed = lax.psum(blocks.astype(jnp.bfloat16), "row").astype(jnp.float32)
    return lax.dynamic_index_in_dim(summed, lax.axis_index("row"), 0, keepdims=False)


def body(right_side, inverse_diag, coupling, pattern):
    levels = right_side.shape[0]
    share_rows = right_side.shape[3]
    rhs_cols = right_side.shape[4]
    block_width = inverse_diag.shape[-1]
    masked = []
    for pair_at in range(levels - 1):
        slab = coupling[pair_at, 0, :, 0, :]
        gate = pattern[pair_at, 0, :, 0, :].astype(jnp.bfloat16)
        shaped = (
            slab.reshape(gate.shape[0], block_width, gate.shape[1], block_width)
            * gate[:, None, :, None]
        )
        masked.append(shaped.reshape(slab.shape))
    panel_spans = [(0, rhs_cols)]
    fwd_levels = []
    for level_at in range(levels):
        pieces = []
        for panel_at, (col_first, col_last) in enumerate(panel_spans):
            source = right_side[level_at, 0, 0, :, col_first:col_last]
            if level_at == 0:
                residual = source
            else:
                partial_value = lift_upward(
                    masked[level_at - 1], fwd_levels[level_at - 1][panel_at][None, None]
                )
                residual = (
                    source.astype(jnp.float32) - forward_sum(partial_value, share_rows)
                ).astype(jnp.bfloat16)
            pieces.append(apply_inverse(inverse_diag[level_at, 0, 0], residual, False))
        fwd_levels.append(pieces)
    bwd_levels = [None] * levels
    for level_at in reversed(range(levels)):
        pieces = []
        panel_at = 0
        known_part = fwd_levels[level_at][panel_at]
        if level_at == levels - 1:
            residual = known_part
        else:
            partial_value = carry_downward(
                masked[level_at], bwd_levels[level_at + 1][panel_at][None, None]
            )
            residual = (
                known_part.astype(jnp.float32) - backward_sum(partial_value, share_rows)
            ).astype(jnp.bfloat16)
        pieces.append(apply_inverse(inverse_diag[level_at, 0, 0], residual, True))
        bwd_levels[level_at] = pieces
    forward_rows = []
    backward_rows = []
    for level_at in range(levels):
        forward_rows.append(jnp.concatenate(fwd_levels[level_at], axis=1))
        backward_rows.append(jnp.concatenate(bwd_levels[level_at], axis=1))
    forward_solution = jnp.stack(forward_rows).reshape(levels, 1, 1, share_rows, rhs_cols)
    solution = jnp.stack(backward_rows).reshape(levels, 1, 1, share_rows, rhs_cols)
    return (forward_solution, solution)


def solution(mesh):
    placed = (
        P(None, "row", ("depth", "col"), None, None),
        P(None, "row", ("depth", "col"), None, None, None),
        P(None, "row", None, ("depth", "col"), None),
        P(None, "row", None, ("depth", "col"), None),
    )
    return jax.shard_map(
        body,
        mesh=mesh,
        in_specs=placed,
        out_specs=(
            P(None, "row", ("depth", "col"), None, None),
            P(None, "row", ("depth", "col"), None, None),
        ),
        check_vma=False,
    )
```

profile of v0, /device:TPU:0, one launch (start us, length us, event | category | flops | bytes accessed | tf_op | source)
XLA Modules:
  0.0 735.9 jit_solution(18099699853977080136)
XLA Ops:
  7.2 0.0 all-gather.13.cloned.1.call-start
  7.2 1.8 convolution_convert_fusion.10
  9.0 0.0 all-gather.13.cloned.1.call-update
  9.0 0.0 all-reduce.7.cloned.1.call-start
  9.0 0.7 convert.11
  9.8 2.6 mul.62
  12.3 7.3 mul.63
  19.6 2.6 mul.71
  22.2 7.3 mul.72
  29.6 2.6 mul.67
  32.2 7.4 mul.68
  39.5 13.6 %slice_multiply_fusion.2 = (bf16[1,1,1024,1,2048]{4,2,3,1,0:T(8,128)(2,1)}, bf16[1,1,1024,1,2048]{4,2,3,1,0:T(8,128)(2,1)}, bf16[1,1,1024,1,2048]{4,2,3,1,0:T(8,128)(2,1)}) fusion(bf16[1,1,1024,1,2048]{4,2,3,1,0:T(8,128)(2,1)} %mul.63, bf16[3,1,1024,1,2048]{4,2,3,1,0:T(8,128)(2,1)} %param.6, bf16[1,1,1024,1,2048]{4,2,3,1,0:T(8,128)(2,1)} %mul.72, ...), kind=kLoop, calls=%fused_computation.8 | loop fusion | flops 6291456 | bytes 37748736 | tf_op jit(solution)/shard_map/mul | solution.py:57
  53.1 5.1 all-gather.13.cloned.1.call-done
  58.2 6.2 fusion.9
  64.5 0.0 all-reduce.7.cloned.1.call-update
  64.5 0.0 all-gather.15.cloned.1.call-start
  64.5 62.1 %all-reduce.7.cloned.1.call-done = bf16[8,128,512]{2,1,0:T(8,128)(2,1)} async-done(((bf16[8,128,512]{2,1,0:T(8,128)(2,1)}), bf16[8,128,512]{2,1,0:T(8,128)(2,1)}) %all-reduce.7.cloned.1.call-update) | async-done | bytes 1048592 | tf_op jit(solution)/shard_map/psum | solution.py:37
  126.6 1.7 convolution_convert_fusion.5
  128.4 0.0 all-gather.15.cloned.1.call-update
  128.4 0.0 all-reduce.9.cloned.1.call-start
  128.5 45.3 %all-gather.15.cloned.1.call-done = bf16[2048,512]{1,0:T(8,128)(2,1)} async-done(((bf16[128,512]{1,0:T(8,128)(2,1)}), bf16[2048,512]{1,0:T(8,128)(2,1)}) %all-gather.15.cloned.1.call-update) | async-done | bytes 2097168 | tf_op jit(solution)/shard_map/all_gather | solution.py:15
  173.7 6.2 fusion.12
  179.9 0.0 all-reduce.9.cloned.1.call-update
  180.0 0.0 all-gather.17.cloned.1.call-start
  180.0 62.1 %all-reduce.9.cloned.1.call-done = bf16[8,128,512]{2,1,0:T(8,128)(2,1)} async-done(((bf16[8,128,512]{2,1,0:T(8,128)(2,1)}), bf16[8,128,512]{2,1,0:T(8,128)(2,1)}) %all-reduce.9.cloned.1.call-update) | async-done | bytes 1048592 | tf_op jit(solution)/shard_map/psum | solution.py:37
  242.1 1.7 convolution_convert_fusion.4
  243.9 0.0 all-gather.17.cloned.1.call-update
  243.9 0.0 all-reduce.11.cloned.1.call-start
  243.9 44.5 %all-gather.17.cloned.1.call-done = bf16[2048,512]{1,0:T(8,128)(2,1)} async-done(((bf16[128,512]{1,0:T(8,128)(2,1)}), bf16[2048,512]{1,0:T(8,128)(2,1)}) %all-gather.17.cloned.1.call-update) | async-done | bytes 2097168 | tf_op jit(solution)/shard_map/all_gather | solution.py:15
  288.5 6.2 fusion.15
  294.7 0.0 all-reduce.11.cloned.1.call-update
  294.7 0.0 all-gather.19.cloned.1.call-start
  294.7 62.1 %all-reduce.11.cloned.1.call-done = bf16[8,128,512]{2,1,0:T(8,128)(2,1)} async-done(((bf16[8,128,512]{2,1,0:T(8,128)(2,1)}), bf16[8,128,512]{2,1,0:T(8,128)(2,1)}) %all-reduce.11.cloned.1.call-update) | async-done | bytes 1048592 | tf_op jit(solution)/shard_map/psum | solution.py:37
  356.8 1.1 convolution_convert_fusion.3
  357.9 0.9 convolution_convert_fusion.9
  358.8 0.0 all-gather.19.cloned.1.call-update
  358.8 0.2 all-reduce.13.cloned.1.call-start
  359.0 15.1 %fusion.2 = (bf16[2048,1024]{0,1:T(8,128)(2,1)}, bf16[2048,1024]{0,1:T(8,128)(2,1)}, bf16[2048,1024]{0,1:T(8,128)(2,1)}) fusion(bf16[128,8,16,128]{3,2,1,0:T(8,128)(2,1)} %bitcast.180, bf16[3,1,1024,1,2048]{4,2,3,1,0:T(8,128)(2,1)} %param.6, bf16[128,8,16,128]{3,2,1,0:T(8,128)(2,1)} %bitcast.182, bf16[128,8,16,128]{3,2,1,0:T(8,128)(2,1)} %bitcast.181), kind=kLoop, calls=%fused_computation.5 | loop fusion | flops 6291456 | bytes 37748736 | tf_op jit(solution)/shard_map/dot_general | solution.py:25
  374.1 6.4 copy.26
  380.5 1.1 all-gather.19.cloned.1.call-done
  381.6 6.3 convolution_convert_fusion.2
  387.9 0.0 all-gather.21.cloned.1.call-start
  387.9 92.3 %all-reduce.13.cloned.1.call-done = bf16[16,128,512]{2,1,0:T(8,128)(2,1)} async-done(((bf16[16,128,512]{2,1,0:T(8,128)(2,1)}), bf16[16,128,512]{2,1,0:T(8,128)(2,1)}) %all-reduce.13.cloned.1.call-update) | async-done | bytes 2097168 | tf_op jit(solution)/shard_map/psum | solution.py:43
  480.2 1.8 convolution_convert_fusion.8
  482.0 0.0 all-gather.21.cloned.1.call-update
  482.0 0.0 all-reduce.15.cloned.1.call-start
  482.1 6.4 copy.25
  488.5 16.4 %all-gather.21.cloned.1.call-done = bf16[1024,512]{0,1:T(8,128)(2,1)} async-done(((bf16[128,512]{0,1:T(8,128)(2,1)}), bf16[1024,512]{0,1:T(8,128)(2,1)}) %all-gather.21.cloned.1.call-update) | async-done | bytes 1048592 | tf_op jit(solution)/shard_map/all_gather | solution.py:23
  504.9 6.3 convolution_convert_fusion.1
  511.2 0.0 all-reduce.15.cloned.1.call-update
  511.2 0.0 all-gather.23.cloned.1.call-start
  511.2 92.3 %all-reduce.15.cloned.1.call-done = bf16[16,128,512]{2,1,0:T(8,128)(2,1)} async-done(((bf16[16,128,512]{2,1,0:T(8,128)(2,1)}), bf16[16,128,512]{2,1,0:T(8,128)(2,1)}) %all-reduce.15.cloned.1.call-update) | async-done | bytes 2097168 | tf_op jit(solution)/shard_map/psum | solution.py:43
  603.5 1.8 convolution_convert_fusion.7
  605.3 0.0 all-gather.23.cloned.1.call-update
  605.3 0.0 all-reduce.17.cloned.1.call-start
  605.3 6.4 copy.24
  611.7 16.4 %all-gather.23.cloned.1.call-done = bf16[1024,512]{0,1:T(8,128)(2,1)} async-done(((bf16[128,512]{0,1:T(8,128)(2,1)}), bf16[1024,512]{0,1:T(8,128)(2,1)}) %all-gather.23.cloned.1.call-update) | async-done | bytes 1048592 | tf_op jit(solution)/shard_map/all_gather | solution.py:23
  628.2 6.3 convolution_convert_fusion
  634.4 0.0 all-reduce.17.cloned.1.call-update
  634.5 0.9 maximum_bitcast_fusion
  635.3 91.5 %all-reduce.17.cloned.1.call-done = bf16[16,128,512]{2,1,0:T(8,128)(2,1)} async-done(((bf16[16,128,512]{2,1,0:T(8,128)(2,1)}), bf16[16,128,512]{2,1,0:T(8,128)(2,1)}) %all-reduce.17.cloned.1.call-update) | async-done | bytes 2097168 | tf_op jit(solution)/shard_map/psum | solution.py:43
  726.8 1.1 fusion.18
  728.0 0.1 maximum_bitcast_fusion.1
  728.1 1.0 copy.17
  (18 shorter events, 0.1 us)
Async XLA Ops:
  7.2 51.1 %all-gather.13.cloned.1.call-start = ((), (), s32[]{:S(2)}) async-start(), calls=%async_computation.6 | async-start | bytes 2228224 | tf_op jit(solution)/shard_map/all_gather | solution.py:15
  9.0 117.6 %all-reduce.7.cloned.1.call-start = ((), (), s32[]{:S(2)}) async-start(), calls=%async_computation | async-start | bytes 2097152 | tf_op jit(solution)/shard_map/psum | solution.py:37
  58.2 68.4 %copy-start.6 = (bf16[4,1,1,128,512]{4,3,2,1,0:T(8,128)(2,1)S(1)}, bf16[4,1,1,128,512]{4,3,2,1,0:T(8,128)(2,1)}, u32[]{:S(2)}) copy-start(bf16[4,1,1,128,512]{4,3,2,1,0:T(8,128)(2,1)} %param.4) | copy-start | bytes 1572868
  58.2 68.4 %copy-start.7 = (bf16[4,1,1,1,128,128]{5,4,3,2,1,0:T(8,128)(2,1)S(1)}, bf16[4,1,1,1,128,128]{5,4,3,2,1,0:T(8,128)(2,1)}, u32[]{:S(2)}) copy-start(bf16[4,1,1,1,128,128]{5,4,3,2,1,0:T(8,128)(2,1)} %param.5) | copy-start | bytes 393220
  64.5 109.2 %all-gather.15.cloned.1.call-start = ((), (), s32[]{:S(2)}) async-start(), calls=%async_computation.7 | async-start | bytes 2228224 | tf_op jit(solution)/shard_map/all_gather | solution.py:15
  128.4 113.7 %all-reduce.9.cloned.1.call-start = ((), (), s32[]{:S(2)}) async-start(), calls=%async_computation.1 | async-start | bytes 2097152 | tf_op jit(solution)/shard_map/psum | solution.py:37
  180.0 108.5 %all-gather.17.cloned.1.call-start = ((), (), s32[]{:S(2)}) async-start(), calls=%async_computation.8 | async-start | bytes 2228224 | tf_op jit(solution)/shard_map/all_gather | solution.py:15
  243.9 113.0 %all-reduce.11.cloned.1.call-start = ((), (), s32[]{:S(2)}) async-start(), calls=%async_computation.2 | async-start | bytes 2097152 | tf_op jit(solution)/shard_map/psum | solution.py:37
  294.7 86.9 %all-gather.19.cloned.1.call-start = ((), (), s32[]{:S(2)}) async-start(), calls=%async_computation.9 | async-start | bytes 1179648 | tf_op jit(solution)/shard_map/all_gather | solution.py:23
  358.8 121.4 %all-reduce.13.cloned.1.call-start = ((), (), s32[]{:S(2)}) async-start(), calls=%async_computation.3 | async-start | bytes 4194304 | tf_op jit(solution)/shard_map/psum | solution.py:43
  381.6 98.7 %copy-start.2 = (bf16[512,128]{0,1:T(8,128)(2,1)S(1)}, bf16[512,128]{0,1:T(8,128)(2,1)}, u32[]{:S(2)}) copy-start(bf16[512,128]{0,1:T(8,128)(2,1)} %convolution_convert_fusion.4) | copy-start | bytes 393220
  387.9 117.0 %all-gather.21.cloned.1.call-start = ((), (), s32[]{:S(2)}) async-start(), calls=%async_computation.10 | async-start | bytes 1179648 | tf_op jit(solution)/shard_map/all_gather | solution.py:23
  482.0 121.4 %all-reduce.15.cloned.1.call-start = ((), (), s32[]{:S(2)}) async-start(), calls=%async_computation.4 | async-start | bytes 4194304 | tf_op jit(solution)/shard_map/psum | solution.py:43
  504.9 98.6 %copy-start.1 = (bf16[512,128]{0,1:T(8,128)(2,1)S(1)}, bf16[512,128]{0,1:T(8,128)(2,1)}, u32[]{:S(2)}) copy-start(bf16[512,128]{0,1:T(8,128)(2,1)} %convolution_convert_fusion.5) | copy-start | bytes 393220
  511.2 117.0 %all-gather.23.cloned.1.call-start = ((), (), s32[]{:S(2)}) async-start(), calls=%async_computation.11 | async-start | bytes 1179648 | tf_op jit(solution)/shard_map/all_gather | solution.py:23
  605.3 121.5 %all-reduce.17.cloned.1.call-start = ((), (), s32[]{:S(2)}) async-start(), calls=%async_computation.5 | async-start | bytes 4194304 | tf_op jit(solution)/shard_map/psum | solution.py:43
  628.1 6.3 copy-start
  628.1 99.8 %copy-start.3 = (bf16[512,128]{1,0:T(8,128)(2,1)S(1)}, bf16[512,128]{1,0:T(8,128)(2,1)}, u32[]{:S(2)}) copy-start(bf16[512,128]{1,0:T(8,128)(2,1)} %convolution_convert_fusion.9) | copy-start | bytes 393220
  628.1 99.8 %copy-start.4 = (bf16[512,128]{1,0:T(8,128)(2,1)S(1)}, bf16[512,128]{1,0:T(8,128)(2,1)}, u32[]{:S(2)}) copy-start(bf16[512,128]{1,0:T(8,128)(2,1)} %convolution_convert_fusion.8) | copy-start | bytes 393220
  628.2 99.8 %copy-start.5 = (bf16[512,128]{1,0:T(8,128)(2,1)S(1)}, bf16[512,128]{1,0:T(8,128)(2,1)}, u32[]{:S(2)}) copy-start(bf16[512,128]{1,0:T(8,128)(2,1)} %convolution_convert_fusion.7) | copy-start | bytes 393220
Sparse Core Ops, SparseCore 0:
  10.7 47.4 all-gather.12
  64.6 61.9 all-reduce.6
  129.4 44.3 all-gather.14
  180.1 61.9 all-reduce.8
  244.1 44.3 all-gather.16
  294.8 61.9 all-reduce.10
  358.9 22.6 all-gather.18
  388.0 92.1 all-reduce.12
  482.2 22.6 all-gather.20
  511.3 92.1 all-reduce.14
  605.4 22.6 all-gather.22
  634.6 92.1 all-reduce.16
where the time goes:
time: 737 us; the launch traced here: 736 us
  waiting for transfers between devices  591 us (80%)
  local copies, waits for them, and re-layouts  50 us (7%)
  matrix products  49.3 us (7%)
  other arithmetic  30.3 us (4%)
  between operations  14.3 us (2%)
    psum x3, waiting for transfers between devices, backward_sum(): summed = lax.psum(blocks.astype(jnp.bfloat16), 'row').astype(jnp.float32)  276 us
    psum x3, waiting for transfers between devices, forward_sum(): lax.psum(blocks.astype(jnp.bfloat16), ('depth', 'col')).astype(jnp.float32)  186 us
    all_gather x3, waiting for transfers between devices, lift_upward(): portion = lax.all_gather(share_in, 'row', axis=0, tiled=True)  94.9 us
    all_gather x3, waiting for transfers between devices, carry_downward(): portion = lax.all_gather(share_in, ('depth', 'col'), axis=1, tiled=True)  33.9 us
    mul x6, local copies, waits for them, and re-layouts, body(): slab.reshape(gate.shape[0], block_width, gate.shape[1], block_width)  29.7 us
    dot_general x3, local copies, waits for them, and re-layouts, carry_downward(): lax.dot_general(masked, portion.reshape(span_rows, portion.shape[-1]), ((...  19.2 us
    dot_general x3, matrix products, carry_downward(): lax.dot_general(masked, portion.reshape(span_rows, portion.shape[-1]), ((...  18.8 us
    dot_general x3, matrix products, lift_upward(): jnp.dot(masked, portion.reshape(span_rows, portion.shape[-1]), preferred_...  18.6 us
  transfers between devices with their start and end apart: 12, of which 12 were waited for; matrix products, arithmetic and copies ran while one was open for 11% of the time, Pallas kernels for 0%

commit v1 on v0

--- a/solution.py
+++ b/solution.py
@@ -34,7 +34,9 @@
     blocks = partial_value.reshape(
         lax.axis_size(("depth", "col")), share_rows, partial_value.shape[-1]
     )
-    summed = lax.psum(blocks.astype(jnp.bfloat16), ("depth", "col")).astype(jnp.float32)
+    summed = jnp.sum(lax.all_gather(blocks.astype(jnp.bfloat16), ("depth", "col")), axis=0).astype(
+        jnp.float32
+    )
     return lax.dynamic_index_in_dim(summed, lax.axis_index(("depth", "col")), 0, keepdims=False)
 
 

time: 737 us -> 712 us (0.966)
  waiting for transfers between devices: 591 us -> 554 us
  other arithmetic: 30.3 us -> 45.3 us
    psum x3 -> x0, waiting for transfers between devices: 186 us -> none  [forward_sum(): lax.psum(blocks.astype(jnp.bfloat16), ('depth', 'col')).astype(jnp.float32)]
    all_gather x0 -> x3, waiting for transfers between devices: none -> 147 us  [forward_sum(): lax.all_gather(blocks.astype(jnp.bfloat16), ('depth', 'col'))]
    reduce_sum x0 -> x3, other arithmetic: none -> 15.1 us  [forward_sum(): jnp.sum(lax.all_gather(blocks.astype(jnp.bfloat16), ('depth', 'col')), ax...]
where the time goes in v1:
time: 712 us; the launch traced here: 711 us
  waiting for transfers between devices  554 us (78%)
  local copies, waits for them, and re-layouts  49.9 us (7%)
  matrix products  46.5 us (7%)
  other arithmetic  45.3 us (6%)
  between operations  14.3 us (2%)
    psum x3, waiting for transfers between devices, backward_sum(): summed = lax.psum(blocks.astype(jnp.bfloat16), 'row').astype(jnp.float32)  276 us
    all_gather x3, waiting for transfers between devices, forward_sum(): lax.all_gather(blocks.astype(jnp.bfloat16), ('depth', 'col'))  147 us
    all_gather x3, waiting for transfers between devices, lift_upward(): portion = lax.all_gather(share_in, 'row', axis=0, tiled=True)  95.7 us
    all_gather x3, waiting for transfers between devices, carry_downward(): portion = lax.all_gather(share_in, ('depth', 'col'), axis=1, tiled=True)  34.8 us
    mul x6, local copies, waits for them, and re-layouts, body(): slab.reshape(gate.shape[0], block_width, gate.shape[1], block_width)  29.7 us
    dot_general x3, local copies, waits for them, and re-layouts, carry_downward(): lax.dot_general(masked, portion.reshape(span_rows, portion.shape[-1]), ((...  19.2 us
    dot_general x3, matrix products, carry_downward(): lax.dot_general(masked, portion.reshape(span_rows, portion.shape[-1]), ((...  18.7 us
    dot_general x3, matrix products, lift_upward(): jnp.dot(masked, portion.reshape(span_rows, portion.shape[-1]), preferred_...  18.6 us
  transfers between devices with their start and end apart: 12, of which 12 were waited for; matrix products, arithmetic and copies ran while one was open for 11% of the time, Pallas kernels for 0%

profile of v1, /device:TPU:0, one launch (start us, length us, event | category | flops | bytes accessed | tf_op | source)
XLA Modules:
  0.0 710.7 jit_solution(8129723786512097328)
XLA Ops:
  7.2 0.0 all-gather.19.cloned.1.call-start
  7.2 1.8 convolution_convert_fusion.10
  9.0 0.0 all-gather.19.cloned.1.call-update
  9.0 0.0 all-gather.21.cloned.1.call-start
  9.0 0.7 convert.14
  9.8 2.6 mul.62
  12.4 7.3 %mul.63 = bf16[1,1,1024,1,2048]{4,2,3,1,0:T(8,128)(2,1)} reshape(bf16[8,128,16,128]{3,2,1,0:T(8,128)(2,1)} %mul.62) | data formatting | bytes 8388608 | tf_op jit(solution)/shard_map/mul | solution.py:59
  19.6 2.5 mul.71
  22.2 7.4 %mul.72 = bf16[1,1,1024,1,2048]{4,2,3,1,0:T(8,128)(2,1)} reshape(bf16[8,128,16,128]{3,2,1,0:T(8,128)(2,1)} %mul.71) | data formatting | bytes 8388608 | tf_op jit(solution)/shard_map/mul | solution.py:59
  29.6 2.6 mul.67
  32.1 7.3 %mul.68 = bf16[1,1,1024,1,2048]{4,2,3,1,0:T(8,128)(2,1)} reshape(bf16[8,128,16,128]{3,2,1,0:T(8,128)(2,1)} %mul.67) | data formatting | bytes 8388608 | tf_op jit(solution)/shard_map/mul | solution.py:59
  39.5 13.6 %slice_multiply_fusion.2 = (bf16[1,1,1024,1,2048]{4,2,3,1,0:T(8,128)(2,1)}, bf16[1,1,1024,1,2048]{4,2,3,1,0:T(8,128)(2,1)}, bf16[1,1,1024,1,2048]{4,2,3,1,0:T(8,128)(2,1)}) fusion(bf16[1,1,1024,1,2048]{4,2,3,1,0:T(8,128)(2,1)} %mul.63, bf16[3,1,1024,1,2048]{4,2,3,1,0:T(8,128)(2,1)} %param.6, bf16[1,1,1024,1,2048]{4,2,3,1,0:T(8,128)(2,1)} %mul.72, ...), kind=kLoop, calls=%fused_computation.8 | loop fusion | flops 6291456 | bytes 37748736 | tf_op jit(solution)/shard_map/mul | solution.py:59
  53.1 5.1 all-gather.19.cloned.1.call-done
  58.2 6.2 fusion.9
  64.5 0.0 all-gather.23.cloned.1.call-start
  64.5 49.0 %all-gather.21.cloned.1.call-done = bf16[64,128,512]{2,1,0:T(8,128)(2,1)} async-done(((bf16[8,128,512]{2,1,0:T(8,128)(2,1)}), bf16[64,128,512]{2,1,0:T(8,128)(2,1)}) %all-gather.21.cloned.1.call-update) | async-done | bytes 8388624 | tf_op jit(solution)/shard_map/all_gather | solution.py:37
  113.5 5.1 reduce_sum.36
  118.6 0.9 convolution_convert_fusion.5
  119.5 0.0 all-gather.25.cloned.1.call-start
  119.6 45.3 %all-gather.23.cloned.1.call-done = bf16[2048,512]{1,0:T(8,128)(2,1)} async-done(((bf16[128,512]{1,0:T(8,128)(2,1)}), bf16[2048,512]{1,0:T(8,128)(2,1)}) %all-gather.23.cloned.1.call-update) | async-done | bytes 2097168 | tf_op jit(solution)/shard_map/all_gather | solution.py:15
  164.8 6.2 fusion.12
  171.1 0.0 all-gather.25.cloned.1.call-update
  171.1 0.0 all-gather.27.cloned.1.call-start
  171.1 49.0 %all-gather.25.cloned.1.call-done = bf16[64,128,512]{2,1,0:T(8,128)(2,1)} async-done(((bf16[8,128,512]{2,1,0:T(8,128)(2,1)}), bf16[64,128,512]{2,1,0:T(8,128)(2,1)}) %all-gather.25.cloned.1.call-update) | async-done | bytes 8388624 | tf_op jit(solution)/shard_map/all_gather | solution.py:37
  220.2 5.0 reduce_sum.37
  225.2 0.9 convolution_convert_fusion.4
  226.0 0.0 all-gather.27.cloned.1.call-update
  226.0 0.0 all-gather.29.cloned.1.call-start
  226.1 45.3 %all-gather.27.cloned.1.call-done = bf16[2048,512]{1,0:T(8,128)(2,1)} async-done(((bf16[128,512]{1,0:T(8,128)(2,1)}), bf16[2048,512]{1,0:T(8,128)(2,1)}) %all-gather.27.cloned.1.call-update) | async-done | bytes 2097168 | tf_op jit(solution)/shard_map/all_gather | solution.py:15
  271.4 6.1 fusion.15
  277.5 0.0 all-gather.29.cloned.1.call-update
  277.6 0.2 all-gather.31.cloned.1.call-start
  277.8 48.9 %all-gather.29.cloned.1.call-done = bf16[64,128,512]{2,1,0:T(8,128)(2,1)} async-done(((bf16[8,128,512]{2,1,0:T(8,128)(2,1)}), bf16[64,128,512]{2,1,0:T(8,128)(2,1)}) %all-gather.29.cloned.1.call-update) | async-done | bytes 8388624 | tf_op jit(solution)/shard_map/all_gather | solution.py:37
  326.6 5.0 reduce_sum.38
  331.6 0.2 convolution_convert_fusion.3
  331.8 0.9 convolution_convert_fusion.9
  332.7 0.0 all-gather.31.cloned.1.call-update
  332.7 0.0 all-reduce.4.cloned.1.call-start
  332.8 15.0 %fusion.2 = (bf16[2048,1024]{0,1:T(8,128)(2,1)}, bf16[2048,1024]{0,1:T(8,128)(2,1)}, bf16[2048,1024]{0,1:T(8,128)(2,1)}) fusion(bf16[128,8,16,128]{3,2,1,0:T(8,128)(2,1)} %bitcast.183, bf16[3,1,1024,1,2048]{4,2,3,1,0:T(8,128)(2,1)} %param.6, bf16[128,8,16,128]{3,2,1,0:T(8,128)(2,1)} %bitcast.185, bf16[128,8,16,128]{3,2,1,0:T(8,128)(2,1)} %bitcast.184), kind=kLoop, calls=%fused_computation.5 | loop fusion | flops 6291456 | bytes 37748736 | tf_op jit(solution)/shard_map/dot_general | solution.py:25
  347.8 6.4 copy.38
  354.1 2.2 all-gather.31.cloned.1.call-done
  356.3 6.2 convolution_convert_fusion.2
  362.5 0.0 all-reduce.4.cloned.1.call-update
  362.6 0.0 all-gather.33.cloned.1.call-start
  362.6 92.3 %all-reduce.4.cloned.1.call-done = bf16[16,128,512]{2,1,0:T(8,128)(2,1)} async-done(((bf16[16,128,512]{2,1,0:T(8,128)(2,1)}), bf16[16,128,512]{2,1,0:T(8,128)(2,1)}) %all-reduce.4.cloned.1.call-update) | async-done | bytes 2097168 | tf_op jit(solution)/shard_map/psum | solution.py:45
  454.9 1.8 convolution_convert_fusion.8
  456.7 0.0 all-gather.33.cloned.1.call-update
  456.7 0.0 all-reduce.6.cloned.1.call-start
  456.8 6.3 copy.37
  463.1 16.5 %all-gather.33.cloned.1.call-done = bf16[1024,512]{0,1:T(8,128)(2,1)} async-done(((bf16[128,512]{0,1:T(8,128)(2,1)}), bf16[1024,512]{0,1:T(8,128)(2,1)}) %all-gather.33.cloned.1.call-update) | async-done | bytes 1048592 | tf_op jit(solution)/shard_map/all_gather | solution.py:23
  479.6 6.3 convolution_convert_fusion.1
  485.9 0.0 all-gather.35.cloned.1.call-start
  485.9 92.3 %all-reduce.6.cloned.1.call-done = bf16[16,128,512]{2,1,0:T(8,128)(2,1)} async-done(((bf16[16,128,512]{2,1,0:T(8,128)(2,1)}), bf16[16,128,512]{2,1,0:T(8,128)(2,1)}) %all-reduce.6.cloned.1.call-update) | async-done | bytes 2097168 | tf_op jit(solution)/shard_map/psum | solution.py:45
  578.2 1.8 convolution_convert_fusion.7
  580.0 0.0 all-gather.35.cloned.1.call-update
  580.0 0.3 all-reduce.8.cloned.1.call-start
  580.3 6.5 copy.36
  586.8 16.1 %all-gather.35.cloned.1.call-done = bf16[1024,512]{0,1:T(8,128)(2,1)} async-done(((bf16[128,512]{0,1:T(8,128)(2,1)}), bf16[1024,512]{0,1:T(8,128)(2,1)}) %all-gather.35.cloned.1.call-update) | async-done | bytes 1048592 | tf_op jit(solution)/shard_map/all_gather | solution.py:23
  602.9 6.3 convolution_convert_fusion
  609.2 0.9 maximum_bitcast_fusion
  610.1 91.5 %all-reduce.8.cloned.1.call-done = bf16[16,128,512]{2,1,0:T(8,128)(2,1)} async-done(((bf16[16,128,512]{2,1,0:T(8,128)(2,1)}), bf16[16,128,512]{2,1,0:T(8,128)(2,1)}) %all-reduce.8.cloned.1.call-update) | async-done | bytes 2097168 | tf_op jit(solution)/shard_map/psum | solution.py:45
  701.6 1.1 fusion.18
  702.7 0.1 maximum_bitcast_fusion.1
  702.8 1.0 copy.29
  (21 shorter events, 0.1 us)
Async XLA Ops:
  7.2 51.1 %all-gather.19.cloned.1.call-start = ((), (), s32[]{:S(2)}) async-start(), calls=%async_computation.3 | async-start | bytes 2228224 | tf_op jit(solution)/shard_map/all_gather | solution.py:15
  9.0 104.5 %all-gather.21.cloned.1.call-start = ((), (), s32[]{:S(2)}) async-start(), calls=%async_computation.4 | async-start | bytes 9437184 | tf_op jit(solution)/shard_map/all_gather | solution.py:37
  64.5 100.4 %all-gather.23.cloned.1.call-start = ((), (), s32[]{:S(2)}) async-start(), calls=%async_computation.5 | async-start | bytes 2228224 | tf_op jit(solution)/shard_map/all_gather | solution.py:15
  113.5 5.1 copy-start.6
  113.5 5.1 copy-start.7
  119.5 100.6 %all-gather.25.cloned.1.call-start = ((), (), s32[]{:S(2)}) async-start(), calls=%async_computation.6 | async-start | bytes 9437184 | tf_op jit(solution)/shard_map/all_gather | solution.py:37
  171.1 100.3 %all-gather.27.cloned.1.call-start = ((), (), s32[]{:S(2)}) async-start(), calls=%async_computation.7 | async-start | bytes 2228224 | tf_op jit(solution)/shard_map/all_gather | solution.py:15
  226.0 100.6 %all-gather.29.cloned.1.call-start = ((), (), s32[]{:S(2)}) async-start(), calls=%async_computation.8 | async-start | bytes 9437184 | tf_op jit(solution)/shard_map/all_gather | solution.py:37
  277.6 78.8 %all-gather.31.cloned.1.call-start = ((), (), s32[]{:S(2)}) async-start(), calls=%async_computation.9 | async-start | bytes 1179648 | tf_op jit(solution)/shard_map/all_gather | solution.py:23
  332.7 122.2 %all-reduce.4.cloned.1.call-start = ((), (), s32[]{:S(2)}) async-start(), calls=%async_computation | async-start | bytes 4194304 | tf_op jit(solution)/shard_map/psum | solution.py:45
  356.3 98.6 %copy-start.2 = (bf16[512,128]{0,1:T(8,128)(2,1)S(1)}, bf16[512,128]{0,1:T(8,128)(2,1)}, u32[]{:S(2)}) copy-start(bf16[512,128]{0,1:T(8,128)(2,1)} %convolution_convert_fusion.4) | copy-start | bytes 393220
  362.6 117.0 %all-gather.33.cloned.1.call-start = ((), (), s32[]{:S(2)}) async-start(), calls=%async_computation.10 | async-start | bytes 1179648 | tf_op jit(solution)/shard_map/all_gather | solution.py:23
  456.7 121.5 %all-reduce.6.cloned.1.call-start = ((), (), s32[]{:S(2)}) async-start(), calls=%async_computation.1 | async-start | bytes 4194304 | tf_op jit(solution)/shard_map/psum | solution.py:45
  479.6 98.7 %copy-start.1 = (bf16[512,128]{0,1:T(8,128)(2,1)S(1)}, bf16[512,128]{0,1:T(8,128)(2,1)}, u32[]{:S(2)}) copy-start(bf16[512,128]{0,1:T(8,128)(2,1)} %convolution_convert_fusion.5) | copy-start | bytes 393220
  485.9 117.0 %all-gather.35.cloned.1.call-start = ((), (), s32[]{:S(2)}) async-start(), calls=%async_computation.11 | async-start | bytes 1179648 | tf_op jit(solution)/shard_map/all_gather | solution.py:23
  580.0 121.5 %all-reduce.8.cloned.1.call-start = ((), (), s32[]{:S(2)}) async-start(), calls=%async_computation.2 | async-start | bytes 4194304 | tf_op jit(solution)/shard_map/psum | solution.py:45
  602.9 6.3 copy-start
  602.9 99.8 %copy-start.3 = (bf16[512,128]{1,0:T(8,128)(2,1)S(1)}, bf16[512,128]{1,0:T(8,128)(2,1)}, u32[]{:S(2)}) copy-start(bf16[512,128]{1,0:T(8,128)(2,1)} %convolution_convert_fusion.9) | copy-start | bytes 393220
  602.9 99.8 %copy-start.4 = (bf16[512,128]{1,0:T(8,128)(2,1)S(1)}, bf16[512,128]{1,0:T(8,128)(2,1)}, u32[]{:S(2)}) copy-start(bf16[512,128]{1,0:T(8,128)(2,1)} %convolution_convert_fusion.8) | copy-start | bytes 393220
  602.9 99.8 %copy-start.5 = (bf16[512,128]{1,0:T(8,128)(2,1)S(1)}, bf16[512,128]{1,0:T(8,128)(2,1)}, u32[]{:S(2)}) copy-start(bf16[512,128]{1,0:T(8,128)(2,1)} %convolution_convert_fusion.7) | copy-start | bytes 393220
Sparse Core Ops, SparseCore 0:
  10.7 47.4 all-gather.18
  64.6 48.9 all-gather.20
  119.6 45.1 all-gather.22
  171.2 48.9 all-gather.24
  226.2 45.1 all-gather.26
  277.7 48.9 all-gather.28
  332.8 23.4 all-gather.30
  362.7 92.2 all-reduce.3
  456.9 22.6 all-gather.32
  486.0 92.1 all-reduce.5
  580.2 22.6 all-gather.34
  609.3 92.2 all-reduce.7
